TPU v7x, 32 devices: a whole 2x2x4 slice. The times are simulated.
32 devices in a mesh: dp: 4 (over z), tp: 8 (over y, x, core).
Axes of the slice: x: 2, y: 2, z: 4, core: 2. Of those that a mesh axis runs over, the one named last changes fastest.
Arguments:
- layer_input: bfloat16 [8192, 2048], P(('dp', 'tp')), may hold values from -6 to 6
- segments: int32 [4, 2048], P('dp'), may hold values from 0 to 1, as said below
- norm_gains: float32 [2, 2048], replicated, may hold values from 0.25 to 1.75
- norm_biases: float32 [2, 2048], replicated, may hold values from -2 to 2
- w_qkv: bfloat16 [2048, 3, 2048], P(None, None, 'tp'), may hold values from -0.125 to 0.125
- qv_bias: float32 [2, 2048], P(None, 'tp'), may hold values from -2 to 2
- key_bias: float32 [32, 16], P('tp'), may hold values from -3 to 3
- w_out: bfloat16 [2048, 2048], P('tp'), may hold values from -2 to 2
- w_gate_up: bfloat16 [2048, 2, 5632], P(None, None, 'tp'), may hold values from -0.125 to 0.125
- w_down: bfloat16 [5632, 2048], P('tp'), may hold values from -0.078125 to 0.078125
- out_grad: bfloat16 [8192, 2048], P(('dp', 'tp')), may hold values from -6 to 6
Outputs:
- output: float32 [8192, 2048], P(('dp', 'tp'))
- grad_x: float32 [8192, 2048], P(('dp', 'tp'))
- grad_qkv: float32 [2048, 3, 2048], P(None, None, 'tp')
- grad_qv_bias: float32 [2, 2048], P(None, 'tp')
- grad_key_bias: float32 [32, 16], P('tp')
- grad_out: float32 [2048, 2048], P('tp')
- grad_gate_up: float32 [2048, 2, 5632], P(None, None, 'tp')
- grad_down: float32 [5632, 2048], P('tp')
- grad_gains: float32 [2, 2048], P(None, 'tp')
- grad_biases: float32 [2, 2048], P(None, 'tp')
Inputs may be any that keep to these rules, and one draw needn't show every extreme that they name: `segments`: in each group the ids number the documents from 0 and never fall; every document has 1024 tokens or more.
All inputs are finite; a program needn't handle non-finite values.
Results may differ from a plain program's by a relative error of at most 0.023.
Values may be sent and summed in bfloat16 or wider, within the bound.
A program may use at most 256 MiB of HBM per device.

v0:
```python
import math
import jax
import jax.numpy as jnp
from jax import lax
from jax.sharding import PartitionSpec as P

D = 2048
HEAD_DIM = 64
ROT = 16
EPSILON = 1e-05


def norm_forward(values, gain, shift_bias):
    centre = jnp.mean(values, axis=-1, keepdims=True)
    centred = values - centre
    spread = jnp.mean(centred * centred, axis=-1, keepdims=True)
    inverse = lax.rsqrt(spread + EPSILON)
    normed = centred * inverse
    return (normed * gain + shift_bias, normed, inverse)


def norm_backward(grad_normed, normed, inverse, gain):
    scaled = grad_normed * gain
    inner = jnp.mean(scaled, axis=-1, keepdims=True)
    along = jnp.mean(scaled * normed, axis=-1, keepdims=True)
    return (
        inverse * (scaled - inner - normed * along),
        jnp.sum(grad_normed * normed, axis=0),
        jnp.sum(grad_normed, axis=0),
    )


def rotary_tables(segment_ids):
    places = jnp.arange(segment_ids.shape[0], dtype=jnp.int32)
    starts_here = jnp.concatenate(
        [jnp.ones((1,), dtype=jnp.bool_), segment_ids[1:] != segment_ids[:-1]]
    )
    doc_start = lax.cummax(jnp.where(starts_here, places, 0), axis=0)
    positions = (places - doc_start).astype(jnp.float32)
    halves = ROT // 2
    frequency = jnp.exp(jnp.arange(halves, dtype=jnp.float32) * (-2.0 * math.log(10000.0) / ROT))
    angles = positions[:, None] * frequency[None, :]
    return (jnp.cos(angles)[:, None, :], jnp.sin(angles)[:, None, :])


def rotate(tensor, cosine, sine):
    halves = ROT // 2
    first_half = tensor[..., :halves]
    second_half = tensor[..., halves:ROT]
    return jnp.concatenate(
        [
            first_half * cosine - second_half * sine,
            second_half * cosine + first_half * sine,
            tensor[..., ROT:],
        ],
        axis=-1,
    )


def rotate_back(tensor, cosine, sine):
    halves = ROT // 2
    first_half = tensor[..., :halves]
    second_half = tensor[..., halves:ROT]
    return jnp.concatenate(
        [
            first_half * cosine + second_half * sine,
            second_half * cosine - first_half * sine,
            tensor[..., ROT:],
        ],
        axis=-1,
    )


def contract_rows(left, right):
    return lax.dot_general(
        left, right, (((0,), (0,)), ((), ())), preferred_element_type=jnp.float32
    )


def contract_cols(left, right):
    return lax.dot_general(
        left, right, (((1,), (1,)), ((), ())), preferred_element_type=jnp.float32
    )


def local(
    layer_input,
    segments,
    norm_gains,
    norm_biases,
    w_qkv,
    qv_bias,
    key_bias,
    w_out,
    w_gate_up,
    w_down,
    out_grad,
):
    segment_ids = segments[0]
    group_rows = segment_ids.shape[0]
    local_width = w_qkv.shape[2]
    local_heads = local_width // HEAD_DIM
    local_hidden = w_down.shape[0]
    block_rows = min(512, group_rows)
    blocks = group_rows // block_rows
    scale = HEAD_DIM ** (-0.5)
    places = jnp.arange(group_rows, dtype=jnp.int32)
    cosine, sine = rotary_tables(segment_ids)
    qkv_matrix = w_qkv.reshape(D, 3 * local_width)
    gate_matrix = w_gate_up.reshape(D, 2 * local_hidden)
    x_float = layer_input.astype(jnp.float32)
    normed_one, hat_one, inverse_one = norm_forward(x_float, norm_gains[0], norm_biases[0])
    rows_one = lax.all_gather(normed_one.astype(jnp.bfloat16), "tp", axis=0, tiled=True)
    projected = jnp.dot(rows_one, qkv_matrix, preferred_element_type=jnp.float32).reshape(
        group_rows, 3, local_heads, HEAD_DIM
    )
    key_full = jnp.concatenate(
        [key_bias, jnp.zeros((local_heads, HEAD_DIM - ROT), jnp.float32)], axis=1
    )
    bias_all = jnp.stack(
        [
            qv_bias[0].reshape(local_heads, HEAD_DIM),
            key_full,
            qv_bias[1].reshape(local_heads, HEAD_DIM),
        ]
    )
    projected = projected + bias_all[None]
    queries = rotate(projected[:, 0], cosine, sine).astype(jnp.bfloat16)
    key_rows = rotate(projected[:, 1], cosine, sine).astype(jnp.bfloat16)
    value_rows = projected[:, 2].astype(jnp.bfloat16)
    query_blocks = queries.reshape(blocks, block_rows, local_heads, HEAD_DIM)
    segment_blocks = segment_ids.reshape(blocks, block_rows)
    place_blocks = places.reshape(blocks, block_rows)

    def scores_of(query_block, segment_block, place_block):
        raw = (
            jnp.einsum("bhd,khd->hbk", query_block, key_rows, preferred_element_type=jnp.float32)
            * scale
        )
        visible = (segment_block[:, None] == segment_ids[None, :]) & (
            place_block[:, None] >= places[None, :]
        )
        return jnp.where(visible[None], raw, -jnp.inf)

    def forward_block(item):
        query_block, segment_block, place_block = item
        scores = scores_of(query_block, segment_block, place_block)
        highest = jnp.max(scores, axis=-1, keepdims=True)
        expo = jnp.exp(scores - highest)
        totals = jnp.sum(expo, axis=-1, keepdims=True)
        probs = (expo / totals).astype(jnp.bfloat16)
        mixed = jnp.einsum("hbk,khd->bhd", probs, value_rows, preferred_element_type=jnp.float32)
        return (mixed.astype(jnp.bfloat16), (highest + jnp.log(totals))[..., 0])

    attended, log_totals = lax.map(forward_block, (query_blocks, segment_blocks, place_blocks))
    attended = attended.reshape(group_rows, local_width)
    hidden_state = x_float + lax.psum_scatter(
        jnp.dot(attended, w_out, preferred_element_type=jnp.float32).astype(jnp.bfloat16),
        "tp",
        scatter_dimension=0,
        tiled=True,
    ).astype(jnp.float32)
    normed_two, hat_two, inverse_two = norm_forward(hidden_state, norm_gains[1], norm_biases[1])
    rows_two = lax.all_gather(normed_two.astype(jnp.bfloat16), "tp", axis=0, tiled=True)
    gate_up = jnp.dot(rows_two, gate_matrix, preferred_element_type=jnp.float32).reshape(
        group_rows, 2, local_hidden
    )
    gate_part = gate_up[:, 0]
    up_part = gate_up[:, 1]
    sigmoid_gate = jax.nn.sigmoid(gate_part)
    silu_gate = gate_part * sigmoid_gate
    activation = (silu_gate * up_part).astype(jnp.bfloat16)
    output = hidden_state + lax.psum_scatter(
        jnp.dot(activation, w_down, preferred_element_type=jnp.float32).astype(jnp.bfloat16),
        "tp",
        scatter_dimension=0,
        tiled=True,
    ).astype(jnp.float32)
    grad_float = out_grad.astype(jnp.float32)
    portion = lax.all_gather(out_grad, "tp", axis=0, tiled=True)
    weight_sum = contract_rows(activation, portion)
    grad_act = contract_cols(portion, w_down)
    grad_down, grad_act = (weight_sum, grad_act)
    grad_gate = grad_act * up_part * sigmoid_gate * (1.0 + gate_part * (1.0 - sigmoid_gate))
    grad_up = grad_act * silu_gate
    grad_pair = (
        jnp.stack([grad_gate, grad_up], axis=1)
        .astype(jnp.bfloat16)
        .reshape(group_rows, 2 * local_hidden)
    )
    grad_gate_up = contract_rows(rows_two, grad_pair).reshape(D, 2, local_hidden)
    grad_normed_two = lax.psum_scatter(
        contract_cols(grad_pair, gate_matrix).astype(jnp.bfloat16),
        "tp",
        scatter_dimension=0,
        tiled=True,
    ).astype(jnp.float32)
    back_two, gain_two, shift_two = norm_backward(
        grad_normed_two, hat_two, inverse_two, norm_gains[1]
    )
    grad_hidden = grad_float + back_two
    portion = lax.all_gather(grad_hidden.astype(jnp.bfloat16), "tp", axis=0, tiled=True)
    weight_sum = contract_rows(attended, portion)
    grad_att = contract_cols(portion, w_out)
    grad_out = weight_sum
    grad_blocks = grad_att.astype(jnp.bfloat16).reshape(blocks, block_rows, local_heads, HEAD_DIM)

    def backward_block(running, item):
        grad_keys, grad_values = running
        query_block, grad_block, log_block, segment_block, place_block = item
        scores = scores_of(query_block, segment_block, place_block)
        weights = jnp.exp(scores - log_block[..., None])
        grad_values = grad_values + jnp.einsum(
            "hbk,bhd->khd",
            weights.astype(jnp.bfloat16),
            grad_block,
            preferred_element_type=jnp.float32,
        )
        grad_weights = jnp.einsum(
            "bhd,khd->hbk", grad_block, value_rows, preferred_element_type=jnp.float32
        )
        inner = jnp.sum(weights * grad_weights, axis=-1, keepdims=True)
        grad_scores = (weights * (grad_weights - inner)).astype(jnp.bfloat16)
        grad_query = (
            jnp.einsum("hbk,khd->bhd", grad_scores, key_rows, preferred_element_type=jnp.float32)
            * scale
        )
        grad_keys = (
            grad_keys
            + jnp.einsum(
                "hbk,bhd->khd", grad_scores, query_block, preferred_element_type=jnp.float32
            )
            * scale
        )
        return ((grad_keys, grad_values), grad_query)

    zero_heads = jnp.zeros((group_rows, local_heads, HEAD_DIM), jnp.float32)
    (grad_keys, grad_values), grad_queries = lax.scan(
        backward_block,
        (zero_heads, zero_heads),
        (query_blocks, grad_blocks, log_totals, segment_blocks, place_blocks),
    )
    grad_queries = grad_queries.reshape(group_rows, local_heads, HEAD_DIM)
    grad_projected = jnp.stack(
        [
            rotate_back(grad_queries, cosine, sine),
            rotate_back(grad_keys, cosine, sine),
            grad_values,
        ],
        axis=1,
    ).astype(jnp.bfloat16)
    bias_sums = jnp.sum(grad_projected, axis=0, dtype=jnp.float32)
    grad_qv = jnp.stack([bias_sums[0].reshape(local_width), bias_sums[2].reshape(local_width)])
    grad_key = bias_sums[1][:, :ROT]
    grad_flat = grad_projected.reshape(group_rows, 3 * local_width)
    grad_qkv = contract_rows(rows_one, grad_flat).reshape(D, 3, local_width)
    grad_normed_one = lax.psum_scatter(
        contract_cols(grad_flat, qkv_matrix).astype(jnp.bfloat16),
        "tp",
        scatter_dimension=0,
        tiled=True,
    ).astype(jnp.float32)
    back_one, gain_one, shift_one = norm_backward(
        grad_normed_one, hat_one, inverse_one, norm_gains[0]
    )
    grad_input = grad_hidden + back_one
    gain_grads, shift_grads = (
        lax.psum_scatter(
            jnp.stack([gain_one, gain_two]).astype(jnp.bfloat16),
            "tp",
            scatter_dimension=1,
            tiled=True,
        ).astype(jnp.float32),
        lax.psum_scatter(
            jnp.stack([shift_one, shift_two]).astype(jnp.bfloat16),
            "tp",
            scatter_dimension=1,
            tiled=True,
        ).astype(jnp.float32),
    )
    grad_qkv, grad_qv, grad_key, grad_out, grad_gate_up, grad_down, gain_grads, shift_grads = (
        lax.psum(grad_qkv.astype(jnp.bfloat16), "dp").astype(jnp.float32),
        lax.psum(grad_qv.astype(jnp.bfloat16), "dp").astype(jnp.float32),
        lax.psum(grad_key.astype(jnp.bfloat16), "dp").astype(jnp.float32),
        lax.psum(grad_out.astype(jnp.bfloat16), "dp").astype(jnp.float32),
        lax.psum(grad_gate_up.astype(jnp.bfloat16), "dp").astype(jnp.float32),
        lax.psum(grad_down.astype(jnp.bfloat16), "dp").astype(jnp.float32),
        lax.psum(gain_grads.astype(jnp.bfloat16), "dp").astype(jnp.float32),
        lax.psum(shift_grads.astype(jnp.bfloat16), "dp").astype(jnp.float32),
    )
    return (
        output,
        grad_input,
        grad_qkv,
        grad_qv,
        grad_key,
        grad_out,
        grad_gate_up,
        grad_down,
        gain_grads,
        shift_grads,
    )


def solution(mesh):
    in_specs = (
        P(("dp", "tp"), None),
        P("dp", None),
        P(),
        P(),
        P(None, None, "tp"),
        P(None, "tp"),
        P("tp", None),
        P("tp", None),
        P(None, None, "tp"),
        P("tp", None),
        P(("dp", "tp"), None),
    )
    out_specs = (
        P(("dp", "tp"), None),
        P(("dp", "tp"), None),
        P(None, None, "tp"),
        P(None, "tp"),
        P("tp", None),
        P("tp", None),
        P(None, None, "tp"),
        P("tp", None),
        P(None, "tp"),
        P(None, "tp"),
    )
    return jax.shard_map(local, mesh=mesh, in_specs=in_specs, out_specs=out_specs, check_vma=False)
```

profile of v0, /device:TPU:0, one launch (start us, length us, event | category | flops | bytes accessed | tf_op | source)
XLA Modules:
  0.0 1480.7 jit_solution(10848038059797148822)
XLA Ops:
  23.3 49.9 %all-gather.5.cloned.1.call-done = bf16[2048,2048]{1,0:T(8,128)(2,1)} async-done(((bf16[256,2048]{1,0:T(8,128)(2,1)}), bf16[2048,2048]{1,0:T(8,128)(2,1)}) %all-gather.5.cloned.1.call-update) | async-done | bytes 8388624 | tf_op jit(solution)/shard_map/all_gather | solution.py:113
  88.5 63.9 %while.28 = (s32[]{:T(128)}, bf16[4,512,4,64]{1,3,2,0:T(8,128)(2,1)}, f32[4,4,512]{2,1,0:T(4,128)S(1)}, s32[4,512]{1,0:T(4,128)S(1)}, s32[1,2048]{1,0:T(1,128)S(...) while((s32[]{:T(128)}, ...), condition=%wide.region_7.8_spmd.clone, body=%wide.region_4.7_spmd.clone.sunk | while | flops 1127348224 | bytes 61427864 | solution.py:155
  161.7 71.6 %reduce-scatter.11.cloned.1.call-done = bf16[256,2048]{1,0:T(8,128)(2,1)} async-done(((bf16[2048,2048]{1,0:T(8,128)(2,1)}), bf16[256,2048]{1,0:T(8,128)(2,1)}) %reduce-scatter.11.cloned.1.call-update) | async-done | bytes 1048592 | tf_op jit(solution)/shard_map/reduce_scatter | solution.py:157
  239.6 53.8 %all-gather.7.cloned.1.call-done = bf16[2048,2048]{1,0:T(8,128)(2,1)} async-done(((bf16[256,2048]{1,0:T(8,128)(2,1)}), bf16[2048,2048]{1,0:T(8,128)(2,1)}) %all-gather.7.cloned.1.call-update) | async-done | bytes 8388624 | tf_op jit(solution)/shard_map/all_gather | solution.py:164
  293.4 18.8 %fusion.53 = f32[2048,2,704]{0,2,1:T(8,128)} fusion(bf16[2048,2048]{1,0:T(8,128)(2,1)} %all-gather.7.cloned.1.call-done, bf16[2048,2,704]{0,2,1:T(8,128)(2,1)} %param.23), kind=kOutput, calls=%fused_computation.64 | convolution fusion | flops 11811160064 | bytes 25690112 | tf_op jit(solution)/shard_map/dot_general | solution.py:165
  312.2 37.2 %all-gather.9.cloned.1.call-done = bf16[2048,2048]{1,0:T(8,128)(2,1)} async-done(((bf16[256,2048]{1,0:T(8,128)(2,1)}), bf16[2048,2048]{1,0:T(8,128)(2,1)}) %all-gather.9.cloned.1.call-update) | async-done | bytes 8388624 | tf_op jit(solution)/shard_map/all_gather | solution.py:180
  349.4 12.9 multiply_bitcast_fusion.1
  364.9 17.9 %bitcast_convert_fusion = bf16[2048,2048]{1,0:T(8,128)(2,1)} fusion(bf16[2048,2,704]{0,2,1:T(8,128)(2,1)} %param.23, bf16[2048,1,704]{0,2,1:T(8,128)(2,1)S(1)} %get-tuple-element.303, bf16[2048,1,704]{0,2,1:T(8,128)(2,1)S(1)} %get-tuple-element.302), kind=kOutput, calls=%fused_computation.56 | convolution fusion | flops 11818237952 | bytes 19922944 | tf_op jit(solution)/shard_map/dot_general | solution.py:81
  382.8 71.6 %reduce-scatter.15.cloned.1.call-done = bf16[256,2048]{1,0:T(8,128)(2,1)} async-done(((bf16[2048,2048]{1,0:T(8,128)(2,1)}), bf16[256,2048]{1,0:T(8,128)(2,1)}) %reduce-scatter.15.cloned.1.call-update) | async-done | bytes 1048592 | tf_op jit(solution)/shard_map/reduce_scatter | solution.py:192
  461.6 54.3 %all-gather.11.cloned.1.call-done = bf16[2048,2048]{1,0:T(8,128)(2,1)} async-done(((bf16[256,2048]{1,0:T(8,128)(2,1)}), bf16[2048,2048]{1,0:T(8,128)(2,1)}) %all-gather.11.cloned.1.call-update) | async-done | bytes 8388624 | tf_op jit(solution)/shard_map/all_gather | solution.py:202
  531.4 245.9 %while.29 = (s32[]{:T(128)}, f32[2048,4,64]{0,2,1:T(8,128)}, f32[2048,4,64]{0,2,1:T(8,128)}, f32[4,512,4,64]{1,0,3,2:T(4,128)}, bf16[4,512,4,64]{1,3,2,0:T(8,128...) while((s32[]{:T(128)}, f32[2048,4,64]{0,2,1:T(8,128)}, ...), condition=%wide.region_17.18_spmd.clone, body=%wide.region_15.17_spmd.clone.sunk | while | flops 2753165312 | bytes 233386272 | solution.py:238
  549.3 12.8 multiply_reduce_fusion.3
  562.1 12.2 multiply_convert_fusion.3
  610.8 12.8 multiply_reduce_fusion.3
  623.6 12.2 multiply_convert_fusion.3
  672.3 12.8 multiply_reduce_fusion.3
  685.1 12.2 multiply_convert_fusion.3
  733.8 12.8 multiply_reduce_fusion.3
  825.2 16.2 %fusion.58 = bf16[2048,2,704]{0,2,1:T(8,128)(2,1)} fusion(bf16[2048,2048]{1,0:T(8,128)(2,1)} %all-gather.7.cloned.1.call-done, bf16[2048,1,704]{0,2,1:T(8,128)(2,1)S(1)} %copy-done.47, bf16[2048,1,704]{0,2,1:T(8,128)(2,1)S(1)} %copy-done.45), kind=kOutput, calls=%fused_computation.79 | convolution fusion | flops 11825577984 | bytes 19922944 | tf_op jit(solution)/shard_map/dot_general | solution.py:75
  854.5 14.9 %reduce-scatter.17.cloned.1.call-done = bf16[256,2048]{1,0:T(8,128)(2,1)} async-done(((bf16[2048,2048]{1,0:T(8,128)(2,1)}), bf16[256,2048]{1,0:T(8,128)(2,1)}) %reduce-scatter.17.cloned.1.call-update) | async-done | bytes 1048592 | tf_op jit(solution)/shard_map/reduce_scatter | solution.py:257
  883.5 61.5 %reduce-scatter.13.cloned.1.call-done = bf16[256,2048]{1,0:T(8,128)(2,1)} async-done(((bf16[2048,2048]{1,0:T(8,128)(2,1)}), bf16[256,2048]{1,0:T(8,128)(2,1)}) %reduce-scatter.13.cloned.1.call-update) | async-done | bytes 1048592 | tf_op jit(solution)/shard_map/reduce_scatter | solution.py:173
  950.3 32.5 %reduce-scatter.19.cloned.1.call-done = bf16[256,2]{1,0:T(8,128)(2,1)} async-done(((bf16[2048,2]{1,0:T(8,128)(2,1)}), bf16[256,2]{1,0:T(8,128)(2,1)}) %reduce-scatter.19.cloned.1.call-update) | async-done | bytes 1040
  983.7 36.2 %reduce-scatter.21.cloned.1.call-done = bf16[256,2]{1,0:T(8,128)(2,1)} async-done(((bf16[2048,2]{1,0:T(8,128)(2,1)}), bf16[256,2]{1,0:T(8,128)(2,1)}) %reduce-scatter.21.cloned.1.call-update) | async-done | bytes 1040
  1035.0 423.0 %all-reduce.5.cloned.1.call-done = (bf16[2048,3,256]{2,0,1:T(8,128)(2,1)}, bf16[256,2048]{1,0:T(8,128)(2,1)}, bf16[2048,2,704]{0,2,1:T(8,128)(2,1)}, bf16[704,2048]{1,0:T(8,128)(2,1)}) async-done(((bf16[2048,3,256]{2,0,1:T(8,128)(2,1)}, bf16[256,2048]{1,0:T(8,128)(2,1)}, bf16[2048,2,704]{0,2,1:T(8,128)(2,1)}, bf16[704,2048]{1,0:T(8,128)(2,1)}), (bf16[2048,3,256]{2,0,1:T(8,128)(2,1)}, ...) | async-done | bytes 12845072 | tf_op jit(solution)/shard_map/psum | solution.py:282
  (311 shorter events, 405.0 us)
Async XLA Ops:
  7.2 342.3 %copy-start = (bf16[704,2048]{1,0:T(8,128)(2,1)S(1)}, bf16[704,2048]{1,0:T(8,128)(2,1)}, u32[]{:S(2)}) copy-start(bf16[704,2048]{1,0:T(8,128)(2,1)} %param.24) | copy-start | bytes 8650756
  7.2 66.0 %all-gather.5.cloned.1.call-start = ((), (), s32[]{:S(2)}) async-start(), calls=%async_computation.6 | async-start | bytes 9437184 | tf_op jit(solution)/shard_map/all_gather | solution.py:113
  16.0 217.2 %reduce-scatter.11.cloned.1.call-start = ((), (), s32[]{:S(2)}) async-start(), calls=%async_computation.7 | async-start | bytes 9437184 | tf_op jit(solution)/shard_map/reduce_scatter | solution.py:157
  23.3 61.6 %copy-start.20 = (f32[2048,8]{0,1:T(8,128)}, f32[2048,8]{0,1:T(8,128)S(1)}, u32[]{:S(2)}) copy-start(f32[2048,8]{0,1:T(8,128)S(1)} %get-tuple-element.324) | copy-start | bytes 196612
  23.3 61.6 %copy-start.22 = (f32[2048,8]{0,1:T(8,128)}, f32[2048,8]{0,1:T(8,128)S(1)}, u32[]{:S(2)}) copy-start(f32[2048,8]{0,1:T(8,128)S(1)} %get-tuple-element.325) | copy-start | bytes 196612
  161.6 75.8 %copy-start.24 = (f32[1,2048]{1,0:T(1,128)S(1)}, f32[1,2048]{1,0:T(1,128)}, u32[]{:S(2)}) copy-start(f32[1,2048]{1,0:T(1,128)} %get-tuple-element.321) | copy-start | bytes 24580
  161.6 75.8 %copy-start.30 = (f32[1,2048]{1,0:T(1,128)S(1)}, f32[1,2048]{1,0:T(1,128)}, u32[]{:S(2)}) copy-start(f32[1,2048]{1,0:T(1,128)} %get-tuple-element.323) | copy-start | bytes 24580
  161.7 131.7 %all-gather.7.cloned.1.call-start = ((), (), s32[]{:S(2)}) async-start(), calls=%async_computation.8 | async-start | bytes 9437184 | tf_op jit(solution)/shard_map/all_gather | solution.py:164
  235.3 222.7 %copy-start.28 = (f32[256]{0:T(256)}, f32[256]{0:T(256)S(1)}, u32[]{:S(2)}) copy-start(f32[256]{0:T(256)S(1)} %broadcast_multiply_fusion.4) | copy-start | bytes 3076
  237.4 220.7 %copy-start.33 = (f32[256]{0:T(256)}, f32[256]{0:T(256)S(1)}, u32[]{:S(2)}) copy-start(f32[256]{0:T(256)S(1)} %add_rsqrt_fusion) | copy-start | bytes 3076
  239.0 110.4 %all-gather.9.cloned.1.call-start = ((), (), s32[]{:S(2)}) async-start(), calls=%async_computation.10 | async-start | bytes 9437184 | tf_op jit(solution)/shard_map/all_gather | solution.py:180
  239.6 214.8 %reduce-scatter.15.cloned.1.call-start = ((), (), s32[]{:S(2)}) async-start(), calls=%async_computation.11 | async-start | bytes 9437184 | tf_op jit(solution)/shard_map/reduce_scatter | solution.py:192
  382.8 133.1 %all-gather.11.cloned.1.call-start = ((), (), s32[]{:S(2)}) async-start(), calls=%async_computation.12 | async-start | bytes 9437184 | tf_op jit(solution)/shard_map/all_gather | solution.py:202
  461.5 407.9 %reduce-scatter.17.cloned.1.call-start = ((), (), s32[]{:S(2)}) async-start(), calls=%async_computation.13 | async-start | bytes 9437184 | tf_op jit(solution)/shard_map/reduce_scatter | solution.py:257
  797.8 147.2 %reduce-scatter.13.cloned.1.call-start = ((), (), s32[]{:S(2)}) async-start(), calls=%async_computation.9 | async-start | bytes 9437184 | tf_op jit(solution)/shard_map/reduce_scatter | solution.py:173
  813.7 169.1 %reduce-scatter.19.cloned.1.call-start = ((), (), s32[]{:S(2)}) async-start(), calls=%async_computation.14 | async-start | bytes 589824
  842.9 28.0 %copy-start.27 = (f32[1,2048]{1,0:T(1,128)S(1)}, f32[1,2048]{1,0:T(1,128)}, u32[]{:S(2)}) copy-start(f32[1,2048]{1,0:T(1,128)} %copy-done.26) | copy-start | bytes 24580
  874.5 145.4 %reduce-scatter.21.cloned.1.call-start = ((), (), s32[]{:S(2)}) async-start(), calls=%async_computation.15 | async-start | bytes 589824
  875.6 582.3 %all-reduce.5.cloned.1.call-start = ((), (), s32[]{:S(2)}) async-start(), calls=%async_computation.16 | async-start | bytes 25690112 | tf_op jit(solution)/shard_map/psum | solution.py:282
  883.2 61.7 %copy-start.25 = (f32[1,2048]{1,0:T(1,128)S(1)}, f32[1,2048]{1,0:T(1,128)}, u32[]{:S(2)}) copy-start(f32[1,2048]{1,0:T(1,128)} %get-tuple-element.321) | copy-start | bytes 24580
  883.2 61.7 %copy-start.29 = (f32[256]{0:T(256)S(1)}, f32[256]{0:T(256)}, u32[]{:S(2)}) copy-start(f32[256]{0:T(256)} %copy-done.28) | copy-start | bytes 3076
  883.2 61.7 %copy-start.34 = (f32[256]{0:T(256)S(1)}, f32[256]{0:T(256)}, u32[]{:S(2)}) copy-start(f32[256]{0:T(256)} %copy-done.33) | copy-start | bytes 3076
  883.2 61.7 %copy-start.39 = (f32[256]{0:T(256)S(1)}, f32[256]{0:T(256)}, u32[]{:S(2)}) copy-start(f32[256]{0:T(256)} %copy-done.38) | copy-start | bytes 3076
  883.2 61.7 %copy-start.41 = (f32[256]{0:T(256)S(1)}, f32[256]{0:T(256)}, u32[]{:S(2)}) copy-start(f32[256]{0:T(256)} %copy-done.40) | copy-start | bytes 3076
  (52 other events, 310.2 us)
Sparse Core Ops, SparseCore 0:
  16.2 56.9 all-gather.4
  161.8 71.4 reduce-scatter.10
  239.1 54.2 all-gather.6
  295.1 54.2 all-gather.8
  382.9 71.4 reduce-scatter.14
  461.6 54.2 all-gather.10
  797.9 71.4 reduce-scatter.16
  873.4 71.4 reduce-scatter.12
  948.6 34.1 reduce-scatter.18
  985.7 34.1 reduce-scatter.20
  1023.3 434.5 all-reduce.4
where the time goes:
time: 1490 us; the launch traced here: 1480 us
  waiting for transfers between devices  907 us (61%)
  matrix products  296 us (20%)
  other arithmetic  133 us (9%)
  local copies, waits for them, and re-layouts  116 us (8%)
    psum x1, waiting for transfers between devices, local(): lax.psum(grad_qkv.astype(jnp.bfloat16), 'dp').astype(jnp.float32)  423 us
    reduce_scatter x1, waiting for transfers between devices, local(): lax.psum_scatter(contract_cols(grad_pair, gate_matrix).astype(jnp.bfloat1...  71.6 us
    reduce_scatter x1, waiting for transfers between devices, local(): lax.psum_scatter(jnp.dot(attended, w_out, preferred_element_type=jnp.floa...  71.6 us
    unnamed x13, waiting for transfers between devices  69.3 us
    reduce_scatter x1, waiting for transfers between devices, local(): lax.psum_scatter(jnp.dot(activation, w_down, preferred_element_type=jnp.f...  61.5 us
    all_gather x1, waiting for transfers between devices, local(): lax.all_gather(grad_hidden.astype(jnp.bfloat16), 'tp', axis=0, tiled=True)  54.3 us
    all_gather x1, waiting for transfers between devices, local(): lax.all_gather(normed_two.astype(jnp.bfloat16), 'tp', axis=0, tiled=True)  53.8 us
    dot_general x4, matrix products, backward_block(): jnp.einsum('bhd,khd->hbk', grad_block, value_rows, preferred_element_type...  51.2 us
  transfers between devices with their start and end apart: 11, of which 11 were waited for; matrix products, arithmetic and copies ran while one was open for 7% of the time, Pallas kernels for 0%

commit v1 on v0

--- a/solution.py
+++ b/solution.py
@@ -279,7 +279,7 @@
         ).astype(jnp.float32),
     )
     grad_qkv, grad_qv, grad_key, grad_out, grad_gate_up, grad_down, gain_grads, shift_grads = (
-        lax.psum(grad_qkv.astype(jnp.bfloat16), "dp").astype(jnp.float32),
+        jnp.sum(lax.all_gather(grad_qkv.astype(jnp.bfloat16), "dp"), axis=0).astype(jnp.float32),
         lax.psum(grad_qv.astype(jnp.bfloat16), "dp").astype(jnp.float32),
         lax.psum(grad_key.astype(jnp.bfloat16), "dp").astype(jnp.float32),
         lax.psum(grad_out.astype(jnp.bfloat16), "dp").astype(jnp.float32),

time: 1490 us -> 1610 us (1.081)
  waiting for transfers between devices: 907 us -> 1010 us
    all_gather x0 -> x1, waiting for transfers between devices: none -> 204 us  [local(): lax.all_gather(grad_qkv.astype(jnp.bfloat16), 'dp')]
    psum x1, waiting for transfers between devices: 423 us -> 318 us  [local(): lax.psum(grad_out.astype(jnp.bfloat16), 'dp').astype(jnp.float32)]
    unnamed x13 -> x14, waiting for transfers between devices: 69.3 us -> 68.7 us
  transfers between devices with their start and end apart: 11 -> 12, of which waited for: 11 -> 12; matrix products, arithmetic and copies ran while one was open for 7% -> 8% of each run, Pallas kernels for 0% -> 0%
where the time goes in v1:
time: 1610 us; the launch traced here: 1600 us
  waiting for transfers between devices  1010 us (63%)
  matrix products  307 us (19%)
  other arithmetic  145 us (9%)
  local copies, waits for them, and re-layouts  117 us (7%)
    psum x1, waiting for transfers between devices, local(): lax.psum(grad_out.astype(jnp.bfloat16), 'dp').astype(jnp.float32)  318 us
    all_gather x1, waiting for transfers between devices, local(): lax.all_gather(grad_qkv.astype(jnp.bfloat16), 'dp')  204 us
    reduce_scatter x1, waiting for transfers between devices, local(): lax.psum_scatter(contract_cols(grad_pair, gate_matrix).astype(jnp.bfloat1...  71.6 us
    reduce_scatter x1, waiting for transfers between devices, local(): lax.psum_scatter(jnp.dot(attended, w_out, preferred_element_type=jnp.floa...  71.6 us
    unnamed x14, waiting for transfers between devices  68.7 us
    reduce_scatter x1, waiting for transfers between devices, local(): lax.psum_scatter(jnp.dot(activation, w_down, preferred_element_type=jnp.f...  60.6 us
    dot_general x4, matrix products, contract_cols(): lax.dot_general(left, right, (((1,), (1,)), ((), ())), preferred_element_...  55.5 us
    all_gather x1, waiting for transfers between devices, local(): lax.all_gather(grad_hidden.astype(jnp.bfloat16), 'tp', axis=0, tiled=True)  54.3 us
  transfers between devices with their start and end apart: 12, of which 12 were waited for; matrix products, arithmetic and copies ran while one was open for 8% of the time, Pallas kernels for 0%

profile of v1, /device:TPU:0, one launch (start us, length us, event | category | flops | bytes accessed | tf_op | source)
XLA Modules:
  0.0 1604.3 jit_solution(6956849473564351153)
XLA Ops:
  23.3 49.9 %all-gather.7.cloned.1.call-done = bf16[2048,2048]{1,0:T(8,128)(2,1)} async-done(((bf16[256,2048]{1,0:T(8,128)(2,1)}), bf16[2048,2048]{1,0:T(8,128)(2,1)}) %all-gather.7.cloned.1.call-update) | async-done | bytes 8388624 | tf_op jit(solution)/shard_map/all_gather | solution.py:113
  88.6 64.0 %while.28 = (s32[]{:T(128)}, bf16[4,512,4,64]{1,3,2,0:T(8,128)(2,1)}, f32[4,4,512]{2,1,0:T(4,128)S(1)}, s32[4,512]{1,0:T(4,128)S(1)}, s32[1,2048]{1,0:T(1,128)S(...) while((s32[]{:T(128)}, ...), condition=%wide.region_7.8_spmd.clone, body=%wide.region_4.7_spmd.clone.sunk | while | flops 1127348224 | bytes 61427864 | solution.py:155
  161.8 71.6 %reduce-scatter.11.cloned.1.call-done = bf16[256,2048]{1,0:T(8,128)(2,1)} async-done(((bf16[2048,2048]{1,0:T(8,128)(2,1)}), bf16[256,2048]{1,0:T(8,128)(2,1)}) %reduce-scatter.11.cloned.1.call-update) | async-done | bytes 1048592 | tf_op jit(solution)/shard_map/reduce_scatter | solution.py:157
  239.8 53.8 %all-gather.9.cloned.1.call-done = bf16[2048,2048]{1,0:T(8,128)(2,1)} async-done(((bf16[256,2048]{1,0:T(8,128)(2,1)}), bf16[2048,2048]{1,0:T(8,128)(2,1)}) %all-gather.9.cloned.1.call-update) | async-done | bytes 8388624 | tf_op jit(solution)/shard_map/all_gather | solution.py:164
  293.6 18.8 %fusion.53 = f32[2048,2,704]{0,2,1:T(8,128)} fusion(bf16[2048,2048]{1,0:T(8,128)(2,1)} %all-gather.9.cloned.1.call-done, bf16[2048,2,704]{0,2,1:T(8,128)(2,1)} %param.23), kind=kOutput, calls=%fused_computation.64 | convolution fusion | flops 11811160064 | bytes 25690112 | tf_op jit(solution)/shard_map/dot_general | solution.py:165
  312.4 37.2 %all-gather.11.cloned.1.call-done = bf16[2048,2048]{1,0:T(8,128)(2,1)} async-done(((bf16[256,2048]{1,0:T(8,128)(2,1)}), bf16[2048,2048]{1,0:T(8,128)(2,1)}) %all-gather.11.cloned.1.call-update) | async-done | bytes 8388624 | tf_op jit(solution)/shard_map/all_gather | solution.py:180
  349.6 12.9 multiply_bitcast_fusion.1
  365.0 26.4 %bitcast_convert_fusion = bf16[2048,2048]{1,0:T(8,128)(2,1)} fusion(bf16[2048,2,704]{0,2,1:T(8,128)(2,1)} %param.23, bf16[2048,1,704]{0,2,1:T(8,128)(2,1)S(1)} %get-tuple-element.302, bf16[2048,1,704]{0,2,1:T(8,128)(2,1)S(1)} %get-tuple-element.301), kind=kOutput, calls=%fused_computation.56 | convolution fusion | flops 11818237952 | bytes 19922944 | tf_op jit(solution)/shard_map/dot_general | solution.py:81
  391.5 71.6 %reduce-scatter.15.cloned.1.call-done = bf16[256,2048]{1,0:T(8,128)(2,1)} async-done(((bf16[2048,2048]{1,0:T(8,128)(2,1)}), bf16[256,2048]{1,0:T(8,128)(2,1)}) %reduce-scatter.15.cloned.1.call-update) | async-done | bytes 1048592 | tf_op jit(solution)/shard_map/reduce_scatter | solution.py:192
  470.3 54.3 %all-gather.13.cloned.1.call-done = bf16[2048,2048]{1,0:T(8,128)(2,1)} async-done(((bf16[256,2048]{1,0:T(8,128)(2,1)}), bf16[2048,2048]{1,0:T(8,128)(2,1)}) %all-gather.13.cloned.1.call-update) | async-done | bytes 8388624 | tf_op jit(solution)/shard_map/all_gather | solution.py:202
  540.1 246.3 %while.29 = (s32[]{:T(128)}, f32[2048,4,64]{0,2,1:T(8,128)}, f32[2048,4,64]{0,2,1:T(8,128)}, f32[4,512,4,64]{1,0,3,2:T(4,128)}, bf16[4,512,4,64]{1,3,2,0:T(8,128...) while((s32[]{:T(128)}, f32[2048,4,64]{0,2,1:T(8,128)}, ...), condition=%wide.region_17.18_spmd.clone, body=%wide.region_15.17_spmd.clone.sunk | while | flops 2753165312 | bytes 233386272 | solution.py:238
  558.2 12.8 multiply_reduce_fusion.3
  571.1 12.2 multiply_convert_fusion.3
  619.8 12.8 multiply_reduce_fusion.3
  681.3 12.8 multiply_reduce_fusion.3
  742.9 12.8 multiply_reduce_fusion.3
  813.8 12.6 convolution_convert_fusion.3
  826.4 16.1 %fusion.58 = bf16[2048,2,704]{0,2,1:T(8,128)(2,1)} fusion(bf16[2048,2048]{1,0:T(8,128)(2,1)S(1)} %bitcast.264, bf16[2048,1,704]{0,2,1:T(8,128)(2,1)} %copy-done.46, bf16[2048,1,704]{0,2,1:T(8,128)(2,1)S(1)} %copy-done.45), kind=kOutput, calls=%fused_computation.79 | convolution fusion | flops 11825577984 | bytes 19922944 | tf_op jit(solution)/shard_map/dot_general | solution.py:75
  862.2 16.3 %reduce-scatter.17.cloned.1.call-done = bf16[256,2048]{1,0:T(8,128)(2,1)} async-done(((bf16[2048,2048]{1,0:T(8,128)(2,1)}), bf16[256,2048]{1,0:T(8,128)(2,1)}) %reduce-scatter.17.cloned.1.call-update) | async-done | bytes 1048592 | tf_op jit(solution)/shard_map/reduce_scatter | solution.py:257
  897.0 318.1 %all-reduce.5.cloned.1.call-done = (bf16[256,2048]{1,0:T(8,128)(2,1)}, bf16[2048,2,704]{0,2,1:T(8,128)(2,1)}, bf16[704,2048]{1,0:T(8,128)(2,1)}) async-done(((bf16[256,2048]{1,0:T(8,128)(2,1)}, bf16[2048,2,704]{0,2,1:T(8,128)(2,1)}, bf16[704,2048]{1,0:T(8,128)(2,1)}), (bf16[256,2048]{1,0:T(8,128)(2,1)}, bf16[2048,2,704]{0,2,1:T(8,128)(2,1)}, bf16[704,2048]{1,0:T(8,128)(2,1)})) %all-reduce.5.cloned.1.call-update) | async-done | bytes 9699344 | tf_op jit(solution)/shard_map/psum | solution.py:285
  1228.4 60.6 %reduce-scatter.13.cloned.1.call-done = bf16[256,2048]{1,0:T(8,128)(2,1)} async-done(((bf16[2048,2048]{1,0:T(8,128)(2,1)}), bf16[256,2048]{1,0:T(8,128)(2,1)}) %reduce-scatter.13.cloned.1.call-update) | async-done | bytes 1048592 | tf_op jit(solution)/shard_map/reduce_scatter | solution.py:173
  1294.4 31.7 %reduce-scatter.19.cloned.1.call-done = bf16[256,2]{1,0:T(8,128)(2,1)} async-done(((bf16[2048,2]{1,0:T(8,128)(2,1)}), bf16[256,2]{1,0:T(8,128)(2,1)}) %reduce-scatter.19.cloned.1.call-update) | async-done | bytes 1040
  1327.0 36.3 %reduce-scatter.21.cloned.1.call-done = bf16[256,2]{1,0:T(8,128)(2,1)} async-done(((bf16[2048,2]{1,0:T(8,128)(2,1)}), bf16[256,2]{1,0:T(8,128)(2,1)}) %reduce-scatter.21.cloned.1.call-update) | async-done | bytes 1040
  1378.4 204.5 %all-gather.15.cloned.1.call-done = bf16[8192,3,256]{2,0,1:T(8,128)(2,1)} async-done(((bf16[2048,3,256]{2,0,1:T(8,128)(2,1)}), bf16[8192,3,256]{2,0,1:T(8,128)(2,1)}) %all-gather.15.cloned.1.call-update) | async-done | bytes 12582928 | tf_op jit(solution)/shard_map/all_gather | solution.py:282
  (318 shorter events, 431.5 us)
Async XLA Ops:
  7.2 342.4 %copy-start = (bf16[704,2048]{1,0:T(8,128)(2,1)S(1)}, bf16[704,2048]{1,0:T(8,128)(2,1)}, u32[]{:S(2)}) copy-start(bf16[704,2048]{1,0:T(8,128)(2,1)} %param.24) | copy-start | bytes 8650756
  7.2 66.0 %all-gather.7.cloned.1.call-start = ((), (), s32[]{:S(2)}) async-start(), calls=%async_computation.6 | async-start | bytes 9437184 | tf_op jit(solution)/shard_map/all_gather | solution.py:113
  16.1 217.4 %reduce-scatter.11.cloned.1.call-start = ((), (), s32[]{:S(2)}) async-start(), calls=%async_computation.7 | async-start | bytes 9437184 | tf_op jit(solution)/shard_map/reduce_scatter | solution.py:157
  23.3 61.6 %copy-start.20 = (f32[2048,8]{0,1:T(8,128)}, f32[2048,8]{0,1:T(8,128)S(1)}, u32[]{:S(2)}) copy-start(f32[2048,8]{0,1:T(8,128)S(1)} %get-tuple-element.323) | copy-start | bytes 196612
  23.3 61.6 %copy-start.22 = (f32[2048,8]{0,1:T(8,128)}, f32[2048,8]{0,1:T(8,128)S(1)}, u32[]{:S(2)}) copy-start(f32[2048,8]{0,1:T(8,128)S(1)} %get-tuple-element.324) | copy-start | bytes 196612
  161.8 75.8 %copy-start.24 = (f32[1,2048]{1,0:T(1,128)S(1)}, f32[1,2048]{1,0:T(1,128)}, u32[]{:S(2)}) copy-start(f32[1,2048]{1,0:T(1,128)} %get-tuple-element.320) | copy-start | bytes 24580
  161.8 75.8 %copy-start.30 = (f32[1,2048]{1,0:T(1,128)S(1)}, f32[1,2048]{1,0:T(1,128)}, u32[]{:S(2)}) copy-start(f32[1,2048]{1,0:T(1,128)} %get-tuple-element.322) | copy-start | bytes 24580
  161.8 131.8 %all-gather.9.cloned.1.call-start = ((), (), s32[]{:S(2)}) async-start(), calls=%async_computation.8 | async-start | bytes 9437184 | tf_op jit(solution)/shard_map/all_gather | solution.py:164
  235.5 231.3 %copy-start.28 = (f32[256]{0:T(256)}, f32[256]{0:T(256)S(1)}, u32[]{:S(2)}) copy-start(f32[256]{0:T(256)S(1)} %broadcast_multiply_fusion.4) | copy-start | bytes 3076
  237.5 229.2 %copy-start.33 = (f32[256]{0:T(256)}, f32[256]{0:T(256)S(1)}, u32[]{:S(2)}) copy-start(f32[256]{0:T(256)S(1)} %add_rsqrt_fusion) | copy-start | bytes 3076
  239.1 110.4 %all-gather.11.cloned.1.call-start = ((), (), s32[]{:S(2)}) async-start(), calls=%async_computation.10 | async-start | bytes 9437184 | tf_op jit(solution)/shard_map/all_gather | solution.py:180
  239.7 223.4 %reduce-scatter.15.cloned.1.call-start = ((), (), s32[]{:S(2)}) async-start(), calls=%async_computation.11 | async-start | bytes 9437184 | tf_op jit(solution)/shard_map/reduce_scatter | solution.py:192
  391.5 133.2 %all-gather.13.cloned.1.call-start = ((), (), s32[]{:S(2)}) async-start(), calls=%async_computation.12 | async-start | bytes 9437184 | tf_op jit(solution)/shard_map/all_gather | solution.py:202
  470.2 408.2 %reduce-scatter.17.cloned.1.call-start = ((), (), s32[]{:S(2)}) async-start(), calls=%async_computation.13 | async-start | bytes 9437184 | tf_op jit(solution)/shard_map/reduce_scatter | solution.py:257
  806.8 408.2 %all-reduce.5.cloned.1.call-start = ((), (), s32[]{:S(2)}) async-start(), calls=%async_computation.17 | async-start | bytes 19398656 | tf_op jit(solution)/shard_map/psum | solution.py:285
  849.5 439.5 %reduce-scatter.13.cloned.1.call-start = ((), (), s32[]{:S(2)}) async-start(), calls=%async_computation.9 | async-start | bytes 9437184 | tf_op jit(solution)/shard_map/reduce_scatter | solution.py:173
  860.7 465.4 %reduce-scatter.19.cloned.1.call-start = ((), (), s32[]{:S(2)}) async-start(), calls=%async_computation.15 | async-start | bytes 589824
  883.5 479.8 %reduce-scatter.21.cloned.1.call-start = ((), (), s32[]{:S(2)}) async-start(), calls=%async_computation.16 | async-start | bytes 589824
  884.7 698.2 %all-gather.15.cloned.1.call-start = ((), (), s32[]{:S(2)}) async-start(), calls=%async_computation.14 | async-start | bytes 15728640 | tf_op jit(solution)/shard_map/all_gather | solution.py:282
  1221.3 67.7 %copy-start.25 = (f32[1,2048]{1,0:T(1,128)S(1)}, f32[1,2048]{1,0:T(1,128)}, u32[]{:S(2)}) copy-start(f32[1,2048]{1,0:T(1,128)} %get-tuple-element.320) | copy-start | bytes 24580
  1221.3 67.7 %copy-start.29 = (f32[256]{0:T(256)S(1)}, f32[256]{0:T(256)}, u32[]{:S(2)}) copy-start(f32[256]{0:T(256)} %copy-done.28) | copy-start | bytes 3076
  1221.3 67.7 %copy-start.34 = (f32[256]{0:T(256)S(1)}, f32[256]{0:T(256)}, u32[]{:S(2)}) copy-start(f32[256]{0:T(256)} %copy-done.33) | copy-start | bytes 3076
  1221.3 67.7 %copy-start.39 = (f32[256]{0:T(256)S(1)}, f32[256]{0:T(256)}, u32[]{:S(2)}) copy-start(f32[256]{0:T(256)} %copy-done.38) | copy-start | bytes 3076
  1221.4 67.7 %copy-start.41 = (f32[256]{0:T(256)S(1)}, f32[256]{0:T(256)}, u32[]{:S(2)}) copy-start(f32[256]{0:T(256)} %copy-done.40) | copy-start | bytes 3076
  (54 other events, 322.6 us)
Sparse Core Ops, SparseCore 0:
  16.2 56.9 all-gather.6
  161.9 71.4 reduce-scatter.10
  239.3 54.2 all-gather.8
  295.3 54.2 all-gather.10
  391.6 71.4 reduce-scatter.14
  470.3 54.2 all-gather.12
  806.9 71.4 reduce-scatter.16
  881.9 333.1 all-reduce.4
  1218.5 70.4 reduce-scatter.12
  1291.9 34.0 reduce-scatter.18
  1329.2 34.0 reduce-scatter.20
  1364.7 218.1 all-gather.14
